TPU v7x, 32 devices: a whole 2x2x4 slice. The times are simulated.
32 devices in a mesh: band: 16 (over z, y, core), ga: 2 (over x).
Axes of the slice: x: 2, y: 2, z: 4, core: 2. Of those that a mesh axis runs over, the one named last changes fastest.
Arguments:
- orbitals: bfloat16 [2, 16, 160, 128], P(None, 'band', 'ga'), may hold values from -8 to 8, as said below
- potential: float32 [480, 480], P('ga'), may hold values from -2 to 2
- slot_sticks: int32 [160], replicated, may hold values from -1 to 126, as said below
- stick_entries: int32 [160, 128], replicated, may hold values from -1 to 126, as said below
Outputs:
- applied_orbitals: bfloat16 [2, 16, 160, 128], P(None, 'band', 'ga')
- correlation: float32 [2, 16, 16], replicated
- reduced_hamiltonian: float32 [2, 16, 16], replicated
Inputs may be any that keep to these rules, and one draw needn't show every extreme that they name: `slot_sticks`: every gx with |gx| < 64 is held by exactly one slot; the other slots hold -1. Slots t with t // 80 = d are those of index d of ga; on some index of ga all 80 slots hold sticks. `stick_entries`: row t lists, in some order, gz + 63 for every gz with gx^2 + gz^2 < 64^2, gx being the stick of slot t, then -1 to the end of the row; rows of empty slots are all -1. `orbitals`: entries where stick_entries is -1 carry values that are not used.
All inputs are finite; a program needn't handle non-finite values.
Results may differ from a plain program's by a relative error of at most 0.001.
Values may be sent and summed in bfloat16 or wider, within the bound.
A program may use at most 64 MiB of HBM per device.

v0:
```python
import jax
import jax.numpy as jnp
from jax import lax
from jax.sharding import PartitionSpec as P

TWO_PI = 6.283185307179586
HIGHEST_PRECISION = lax.Precision.HIGHEST


def phases(frequency, position, points):
    winding = frequency[:, None] * position[None, :] % points
    angles = winding.astype(jnp.float32) * (TWO_PI / points)
    return (jnp.cos(angles), jnp.sin(angles))


def stick_phases(slot_sticks, radius, points):
    frequency = slot_sticks - radius + 1
    x_cos, x_sin = phases(frequency, jnp.arange(points, dtype=jnp.int32), points)
    filled = (slot_sticks >= 0).astype(jnp.float32)[:, None]
    return (x_cos * filled, x_sin * filled)


def selector_table(entry_lists):
    width = entry_lists.shape[1]
    return (entry_lists[:, :, None] == jnp.arange(width, dtype=jnp.int32)[None, None, :]).astype(
        jnp.bfloat16
    )


def spread_entries(coeffs, selector):
    return jnp.einsum("cbsk,skp->cbsp", coeffs, selector, preferred_element_type=jnp.float32)


def pick_entries(spectra, selector):
    return jnp.einsum(
        "cbsp,skp->cbsk", spectra, selector.astype(jnp.float32), precision=HIGHEST_PRECISION
    )


def z_forward(spread, z_cos, z_sin):
    real_part = jnp.einsum(
        "bsp,pz->bsz", spread[0], z_cos, precision=HIGHEST_PRECISION
    ) - jnp.einsum("bsp,pz->bsz", spread[1], z_sin, precision=HIGHEST_PRECISION)
    imag_part = jnp.einsum(
        "bsp,pz->bsz", spread[0], z_sin, precision=HIGHEST_PRECISION
    ) + jnp.einsum("bsp,pz->bsz", spread[1], z_cos, precision=HIGHEST_PRECISION)
    return jnp.stack([real_part, imag_part])


def plane_work(columns, x_cos, x_sin, potential):
    field_real = jnp.einsum(
        "bsz,sx->bzx", columns[0], x_cos, precision=HIGHEST_PRECISION
    ) - jnp.einsum("bsz,sx->bzx", columns[1], x_sin, precision=HIGHEST_PRECISION)
    field_imag = jnp.einsum(
        "bsz,sx->bzx", columns[0], x_sin, precision=HIGHEST_PRECISION
    ) + jnp.einsum("bsz,sx->bzx", columns[1], x_cos, precision=HIGHEST_PRECISION)
    prod_real = potential[None] * field_real
    prod_imag = potential[None] * field_imag
    back_real = jnp.einsum(
        "bzx,sx->bsz", prod_real, x_cos, precision=HIGHEST_PRECISION
    ) + jnp.einsum("bzx,sx->bsz", prod_imag, x_sin, precision=HIGHEST_PRECISION)
    back_imag = jnp.einsum(
        "bzx,sx->bsz", prod_imag, x_cos, precision=HIGHEST_PRECISION
    ) - jnp.einsum("bzx,sx->bsz", prod_real, x_sin, precision=HIGHEST_PRECISION)
    return jnp.stack([back_real, back_imag])


def z_backward(gathered, z_cos, z_sin, points):
    real_part = jnp.einsum(
        "bsz,pz->bsp", gathered[0], z_cos, precision=HIGHEST_PRECISION
    ) + jnp.einsum("bsz,pz->bsp", gathered[1], z_sin, precision=HIGHEST_PRECISION)
    imag_part = jnp.einsum(
        "bsz,pz->bsp", gathered[1], z_cos, precision=HIGHEST_PRECISION
    ) - jnp.einsum("bsz,pz->bsp", gathered[0], z_sin, precision=HIGHEST_PRECISION)
    return jnp.stack([real_part, imag_part]) / float(points * points)


def kinetic_factor(sticks, entry_lists, radius):
    gx_value = sticks - radius + 1
    gz_value = entry_lists - radius + 1
    return ((gx_value * gx_value)[:, None] + gz_value * gz_value).astype(jnp.float32) / float(
        radius * radius
    )


def cross_products(left, right, scale):
    dims = (((1,), (1,)), ((), ()))
    real_part = lax.dot_general(
        left[0], right[0], dims, preferred_element_type=jnp.float32
    ) + lax.dot_general(left[1], right[1], dims, preferred_element_type=jnp.float32)
    imag_part = lax.dot_general(
        left[0], right[1], dims, preferred_element_type=jnp.float32
    ) - lax.dot_general(left[1], right[0], dims, preferred_element_type=jnp.float32)
    return jnp.stack([real_part, imag_part]) * scale


def body(orbitals, potential, slot_sticks, stick_entries):
    points = potential.shape[1]
    width = stick_entries.shape[1]
    radius = width // 2
    band_count = orbitals.shape[1]
    slot_count = orbitals.shape[2]
    ga_index = lax.axis_index("ga")
    own_first = ga_index * slot_count
    own_lists = lax.dynamic_slice_in_dim(stick_entries, own_first, slot_count, 0)
    own_sticks = lax.dynamic_slice_in_dim(slot_sticks, own_first, slot_count, 0)
    present = own_lists >= 0
    own_selector = selector_table(own_lists)
    masked = jnp.where(present[None, None], orbitals, jnp.zeros_like(orbitals))
    frequency = jnp.arange(width, dtype=jnp.int32) - radius + 1
    whole_cos, whole_sin = phases(frequency, jnp.arange(points, dtype=jnp.int32), points)
    x_cos, x_sin = stick_phases(slot_sticks, radius, points)
    columns = z_forward(spread_entries(orbitals, own_selector), whole_cos, whole_sin)
    planes_columns = lax.all_to_all(columns, "ga", split_axis=3, concat_axis=2, tiled=True)
    gathered = plane_work(planes_columns, x_cos, x_sin, potential)
    returned = lax.all_to_all(gathered, "ga", split_axis=2, concat_axis=3, tiled=True)
    spectra = z_backward(returned, whole_cos, whole_sin, points)
    applied = pick_entries(spectra, own_selector)
    kinetic = kinetic_factor(own_sticks, own_lists, radius)
    applied_orbitals = jnp.where(
        present[None, None],
        kinetic[None, None] * orbitals.astype(jnp.float32) + applied,
        jnp.float32(0.0),
    ).astype(jnp.bfloat16)
    scale = 1.0 / (4.0 * radius * radius)
    flat_psi = masked.reshape(2, band_count, -1)
    flat_h = applied_orbitals.reshape(2, band_count, -1)
    portion = lax.all_gather(masked, "band", axis=1, tiled=True)
    remote_psi = portion.reshape(2, portion.shape[1], -1)
    block = jnp.stack(
        [cross_products(remote_psi, flat_psi, scale), cross_products(remote_psi, flat_h, scale)]
    )
    summed = lax.psum(block, "ga")
    matrices = lax.all_gather(summed, "band", axis=3, tiled=True)
    return (applied_orbitals, matrices[0], matrices[1])


def solution(mesh):
    return jax.shard_map(
        body,
        mesh=mesh,
        in_specs=(P(None, "band", "ga", None), P("ga", None), P(), P()),
        out_specs=(P(None, "band", "ga", None), P(), P()),
        check_vma=False,
    )
```

profile of v0, /device:TPU:0, one launch (start us, length us, event | category | flops | bytes accessed | tf_op | source)
XLA Modules:
  0.0 106.6 jit_solution(10663238395581667539)
XLA Ops:
  0.6 0.8 add_multiply_fusion
  1.4 0.9 convert_multiply_fusion
  2.3 3.0 %fusion.10 = f32[2,1,80,128]{3,0,2,1:T(2,128)S(1)} fusion(s32[80,128]{1,0:T(8,128)S(1)} %get-tuple-element.16, bf16[2,80,128]{2,1,0:T(8,128)(2,1)} %bitcast.158), kind=kOutput, calls=%fused_computation.17 | convolution fusion | flops 6553600 | bytes 163840 | tf_op jit(solution)/shard_map/cbsk,skp->cbsp/dot_general | solution.py:31
  5.3 0.1 fusion.194
  5.3 1.3 %fusion.53 = f32[80,480]{1,0:T(8,128)S(1)} fusion(f32[80,128]{1,0:T(8,128)S(1)} %bitcast.156, s32[128]{0:T(128)S(1)} %iota_add_fusion), kind=kOutput, calls=%fused_computation.76 | convolution fusion | flops 59535360 | bytes 195072 | tf_op jit(solution)/shard_map/bsp,pz->bsz/dot_general | solution.py:41
  6.7 1.4 %fusion.57 = f32[80,480]{1,0:T(8,128)S(1)} fusion(f32[80,128]{1,0:T(8,128)S(1)} %bitcast.157, s32[128]{0:T(128)S(1)} %iota_add_fusion), kind=kOutput, calls=%fused_computation.77 | convolution fusion | flops 59535360 | bytes 195072 | tf_op jit(solution)/shard_map/bsp,pz->bsz/dot_general | solution.py:44
  8.1 1.4 %fusion.9 = f32[1,1,80,480]{3,2,1,0:T(8,128)S(1)} fusion(f32[80,480]{1,0:T(8,128)S(1)} %fusion.53, f32[80,128]{1,0:T(8,128)S(1)} %bitcast.154, s32[128]{0:T(128)S(1)} %iota_add_fusion), kind=kOutput, calls=%fused_computation.16 | convolution fusion | flops 59573760 | bytes 348672 | tf_op jit(solution)/shard_map/bsp,pz->bsz/dot_general | solution.py:43
  9.5 1.4 %fusion.8 = f32[1,1,80,480]{3,2,1,0:T(8,128)S(1)} fusion(f32[80,480]{1,0:T(8,128)S(1)} %fusion.57, f32[80,128]{1,0:T(8,128)S(1)} %bitcast.155, s32[128]{0:T(128)S(1)} %iota_add_fusion), kind=kOutput, calls=%fused_computation.14 | convolution fusion | flops 59573760 | bytes 348672 | tf_op jit(solution)/shard_map/bsp,pz->bsz/dot_general | solution.py:46
  10.8 1.0 copy.37
  11.9 4.4 %all-to-all-start = ((f32[2,1,80,480]{2,1,0,3:T(1,128)}), f32[2,1,80,480]{2,1,0,3:T(1,128)S(1)}, u32[]{:S(2)}, u32[]{:S(2)}) async-start(f32[2,1,80,480]{2,1,0,3:T(1,128)} %copy.37), calls=%async_computation | async-start | bytes 983040 | tf_op jit(solution)/shard_map/all_to_all | solution.py:114
  16.3 0.1 broadcast_select_fusion
  16.4 24.4 %all_gather.6 = bf16[2,16,80,128]{3,2,0,1:T(8,128)(2,1)S(1)} all-gather(bf16[2,1,80,128]{3,2,0,1:T(8,128)(2,1)S(1)} %copy.45), channel_id=1, replica_groups=mesh['band'=16,'ga'=2] {'band'}, dimensions={1}, use_global_device_ids=true | all-gather | bytes 696320 | tf_op jit(solution)/shard_map/all_gather | solution.py:128
  40.8 0.2 convolution_bitcast_fusion.5
  41.1 0.2 fusion.22
  41.3 0.8 copy.50
  42.1 0.1 fusion.193
  42.3 1.9 %fusion.40 = f32[240,480]{1,0:T(8,128)S(1)} fusion(f32[160,240]{1,0:T(8,128)S(1)} %bitcast.152, f32[160]{0:T(256)S(1)} %compare_convert_fusion, s32[160]{0:T(256)S(1)} %broadcast_add_fusion), kind=kOutput, calls=%fused_computation.65 | convolution fusion | flops 221952000 | bytes 615680 | tf_op jit(solution)/shard_map/bsz,sx->bzx/dot_general | solution.py:51
  44.2 1.9 %fusion.41 = f32[240,480]{1,0:T(8,128)S(1)} fusion(f32[160,240]{1,0:T(8,128)S(1)} %bitcast.153, f32[160]{0:T(256)S(1)} %compare_convert_fusion, s32[160]{0:T(256)S(1)} %broadcast_add_fusion), kind=kOutput, calls=%fused_computation.66 | convolution fusion | flops 221952000 | bytes 615680 | tf_op jit(solution)/shard_map/bsz,sx->bzx/dot_general | solution.py:54
  46.1 1.9 %fusion.5 = f32[240,480]{1,0:T(8,128)S(1)} fusion(f32[240,480]{1,0:T(8,128)S(1)} %copy-done, f32[240,480]{1,0:T(8,128)S(1)} %fusion.40, f32[160,240]{1,0:T(8,128)S(1)} %bitcast.139, f32[160]{0:T(256)S(1)} %compare_convert_fusion, s32[160]{0:T(256)S(1)} %broadcast_add_fusion), kind=kOutput, calls=%fused_computation.8 | convolution fusion | flops 222182400 | bytes 1537280 | tf_op jit(solution)/shard_map/bsz,sx->bzx/dot_general | solution.py:53
  48.0 1.9 %fusion.39 = f32[160,240]{1,0:T(8,128)S(1)} fusion(f32[240,480]{1,0:T(8,128)S(1)} %fusion.5, f32[160]{0:T(256)S(1)} %compare_convert_fusion, s32[160]{0:T(256)S(1)} %broadcast_add_fusion), kind=kOutput, calls=%fused_computation.64 | convolution fusion | flops 221952000 | bytes 615680 | tf_op jit(solution)/shard_map/bzx,sx->bsz/dot_general | solution.py:59
  49.9 1.9 %fusion.4 = f32[240,480]{1,0:T(8,128)S(1)} fusion(f32[240,480]{1,0:T(8,128)S(1)} %copy-done, f32[240,480]{1,0:T(8,128)S(1)} %fusion.41, f32[160,240]{1,0:T(8,128)S(1)} %bitcast.140, f32[160]{0:T(256)S(1)} %compare_convert_fusion, s32[160]{0:T(256)S(1)} %broadcast_add_fusion), kind=kOutput, calls=%fused_computation.6 | convolution fusion | flops 222182400 | bytes 1537280 | tf_op jit(solution)/shard_map/bsz,sx->bzx/dot_general | solution.py:56
  51.8 1.9 %fusion.38 = f32[160,240]{1,0:T(8,128)S(1)} fusion(f32[240,480]{1,0:T(8,128)S(1)} %fusion.4, f32[160]{0:T(256)S(1)} %compare_convert_fusion, s32[160]{0:T(256)S(1)} %broadcast_add_fusion), kind=kOutput, calls=%fused_computation.63 | convolution fusion | flops 221952000 | bytes 615680 | tf_op jit(solution)/shard_map/bzx,sx->bsz/dot_general | solution.py:62
  53.7 2.1 %fusion.7 = f32[1,1,160,240]{3,2,1,0:T(8,128)S(1)} fusion(f32[160,240]{1,0:T(8,128)S(1)} %fusion.39, f32[240,480]{1,0:T(8,128)S(1)} %fusion.4, f32[160]{0:T(256)S(1)} %compare_convert_fusion, s32[160]{0:T(256)S(1)} %broadcast_add_fusion), kind=kOutput, calls=%fused_computation.12 | convolution fusion | flops 221990400 | bytes 769280 | tf_op jit(solution)/shard_map/bzx,sx->bsz/dot_general | solution.py:61
  55.9 1.9 %fusion.6 = f32[1,1,160,240]{3,2,1,0:T(8,128)S(1)} fusion(f32[160,240]{1,0:T(8,128)S(1)} %fusion.38, f32[240,480]{1,0:T(8,128)S(1)} %fusion.5, f32[160]{0:T(256)S(1)} %compare_convert_fusion, s32[160]{0:T(256)S(1)} %broadcast_add_fusion), kind=kOutput, calls=%fused_computation.10 | convolution fusion | flops 221990400 | bytes 769280 | tf_op jit(solution)/shard_map/bzx,sx->bsz/dot_general | solution.py:64
  57.8 1.1 copy.41
  58.9 3.5 %all-to-all-start.1 = ((f32[2,1,160,240]{3,1,0,2:T(1,128)}), f32[2,1,160,240]{3,1,0,2:T(1,128)S(1)}, u32[]{:S(2)}, u32[]{:S(2)}) async-start(f32[2,1,160,240]{3,1,0,2:T(1,128)} %copy.41), calls=%async_computation.1 | async-start | bytes 655360 | tf_op jit(solution)/shard_map/all_to_all | solution.py:116
  62.4 0.2 convolution_bitcast_fusion.7
  62.6 0.2 fusion.24
  62.8 6.5 %all-to-all-done.1 = f32[2,1,160,240]{3,1,0,2:T(1,128)S(1)} async-done(((f32[2,1,160,240]{3,1,0,2:T(1,128)}), f32[2,1,160,240]{3,1,0,2:T(1,128)S(1)}, u32[]{:S(2)}, u32[]{:S(2)}) %all-to-all-start.1) | async-done | bytes 307232 | tf_op jit(solution)/shard_map/all_to_all | solution.py:116
  69.3 0.2 copy.51
  69.4 0.3 copy.93
  69.7 0.1 fusion.192
  69.8 0.2 reshape.267
  70.0 1.4 %fusion.50 = f32[80,128]{1,0:T(8,128)S(1)} fusion(f32[80,480]{1,0:T(8,128)S(1)} %reshape.267, s32[128]{0:T(128)S(1)} %iota_add_fusion), kind=kOutput, calls=%fused_computation.75 | convolution fusion | flops 59535360 | bytes 195072 | tf_op jit(solution)/shard_map/bsz,pz->bsp/dot_general | solution.py:69
  71.4 0.2 reshape.268
  71.6 1.4 %fusion.48 = f32[80,128]{1,0:T(8,128)S(1)} fusion(f32[80,480]{1,0:T(8,128)S(1)} %reshape.268, s32[128]{0:T(128)S(1)} %iota_add_fusion), kind=kOutput, calls=%fused_computation.74 | convolution fusion | flops 59535360 | bytes 195072 | tf_op jit(solution)/shard_map/bsz,pz->bsp/dot_general | solution.py:72
  73.0 1.4 %fusion.16 = f32[1,80,128]{2,1,0:T(8,128)S(1)} fusion(f32[80,128]{1,0:T(8,128)S(1)} %fusion.50, f32[80,480]{1,0:T(8,128)S(1)} %reshape.268, s32[128]{0:T(128)S(1)} %iota_add_fusion), kind=kOutput, calls=%fused_computation.25 | convolution fusion | flops 59545600 | bytes 236032 | tf_op jit(solution)/shard_map/bsz,pz->bsp/dot_general | solution.py:71
  74.5 1.5 %fusion.15 = f32[1,80,128]{2,1,0:T(8,128)S(1)} fusion(f32[80,128]{1,0:T(8,128)S(1)} %fusion.48, f32[80,480]{1,0:T(8,128)S(1)} %reshape.267, s32[128]{0:T(128)S(1)} %iota_add_fusion), kind=kOutput, calls=%fused_computation.23 | convolution fusion | flops 59545600 | bytes 236032 | tf_op jit(solution)/shard_map/bsz,pz->bsp/dot_general | solution.py:74
  76.0 5.6 %fusion.14 = bf16[2,1,80,128]{3,0,2,1:T(2,128)(2,1)S(1)} fusion(s32[80,128]{1,0:T(8,128)S(1)} %get-tuple-element.16, f32[2,80,128]{2,1,0:T(8,128)S(1)} %maximum_multiply_fusion, pred[80,128]{1,0:T(8,128)(4,1)S(1)} %broadcast_compare_fusion, f32[80,128]{1,0:T(8,128)S(1)} %get-tuple-element.15, bf16[2,1,80,128]{3,2,1,0:T(8,128)(2,1)S(1)} %copy-done.1), kind=kOutput, calls=%fused_computation.21 | convolution fusion | flops 32870400 | bytes 256000 | tf_op jit(solution)/shard_map/cbsp,skp->cbsk/dot_general | solution.py:35
  81.6 0.2 convolution_bitcast_fusion.3
  81.8 0.2 convolution_bitcast_fusion.1
  82.0 0.6 copy.47
  82.7 0.2 fusion.20
  82.9 0.2 fusion.18
  83.1 4.9 %psum.7 = f32[2,2,16,1]{2,3,1,0:T(1,128)S(1)} all-reduce(f32[2,2,16,1]{2,3,1,0:T(1,128)S(1)} %pad_maximum_fusion.2), channel_id=1, replica_groups=mesh['band'=16,'ga'=2] {'ga'}, use_global_device_ids=true, to_apply=%region_0.1 | all-reduce | flops 64 | bytes 512 | tf_op jit(solution)/shard_map/psum | solution.py:133
  88.1 17.2 %all_gather.7 = f32[2,2,16,16]{2,1,0,3:T(2,128)S(1)} all-gather(f32[2,2,16,1]{2,1,0,3:T(2,128)S(1)} %bitcast.159), channel_id=1, replica_groups=mesh['band'=16,'ga'=2] {'band'}, dimensions={3}, use_global_device_ids=true | all-gather | bytes 4352 | tf_op jit(solution)/shard_map/all_gather | solution.py:134
  105.3 0.7 copy.48
  106.0 0.7 copy.49
  (21 shorter events, 0.2 us)
Async XLA Ops:
  11.9 4.4 %copy-start.2 = (s32[160]{0:T(256)S(1)}, s32[160]{0:T(256)}, u32[]{:S(2)}) copy-start(s32[160]{0:T(256)} %param.6) | copy-start | bytes 1924
  11.9 4.4 %copy-start.1 = (bf16[2,1,80,128]{3,2,1,0:T(8,128)(2,1)S(1)}, bf16[2,1,80,128]{3,2,1,0:T(8,128)(2,1)}, u32[]{:S(2)}) copy-start(bf16[2,1,80,128]{3,2,1,0:T(8,128)(2,1)} %param.4) | copy-start | bytes 122884
  11.9 29.4 %all-to-all-start = ((f32[2,1,80,480]{2,1,0,3:T(1,128)}), f32[2,1,80,480]{2,1,0,3:T(1,128)S(1)}, u32[]{:S(2)}, u32[]{:S(2)}) async-start(f32[2,1,80,480]{2,1,0,3:T(1,128)} %copy.37), calls=%async_computation | async-start | bytes 983040 | tf_op jit(solution)/shard_map/all_to_all | solution.py:114
  44.2 1.9 %copy-start = (f32[240,480]{1,0:T(8,128)S(1)}, f32[240,480]{1,0:T(8,128)}, u32[]{:S(2)}) copy-start(f32[240,480]{1,0:T(8,128)} %param.5) | copy-start | bytes 1382404
  58.9 10.4 %all-to-all-start.1 = ((f32[2,1,160,240]{3,1,0,2:T(1,128)}), f32[2,1,160,240]{3,1,0,2:T(1,128)S(1)}, u32[]{:S(2)}, u32[]{:S(2)}) async-start(f32[2,1,160,240]{3,1,0,2:T(1,128)} %copy.41), calls=%async_computation.1 | async-start | bytes 655360 | tf_op jit(solution)/shard_map/all_to_all | solution.py:116
where the time goes:
time: 107 us
  blocking collectives  46.5 us (43%)
  matrix products  37 us (35%)
  starting transfers between devices  7.82 us (7%)
  waiting for transfers between devices  6.46 us (6%)
  local copies, waits for them, and re-layouts  6.1 us (6%)
  other arithmetic  1.8 us (2%)
    all_gather x1, blocking collectives, body(): portion = lax.all_gather(masked, 'band', axis=1, tiled=True)  24.4 us
    all_gather x1, blocking collectives, body(): matrices = lax.all_gather(summed, 'band', axis=3, tiled=True)  17.2 us
    all_to_all x1, waiting for transfers between devices, body(): lax.all_to_all(gathered, 'ga', split_axis=2, concat_axis=3, tiled=True)  6.46 us
    dot_general x1, matrix products, pick_entries(): jnp.einsum('cbsp,skp->cbsk', spectra, selector.astype(jnp.float32), preci...  5.62 us
    psum x1, blocking collectives, body(): summed = lax.psum(block, 'ga')  4.93 us
    all_to_all x1, starting transfers between devices, body(): lax.all_to_all(columns, 'ga', split_axis=3, concat_axis=2, tiled=True)  4.36 us
    all_to_all x1, starting transfers between devices, body(): lax.all_to_all(gathered, 'ga', split_axis=2, concat_axis=3, tiled=True)  3.45 us
    dot_general x1, matrix products, spread_entries(): jnp.einsum('cbsk,skp->cbsp', coeffs, selector, preferred_element_type=jnp...  3.01 us
  transfers between devices with their start and end apart: 2, of which 1 were waited for; matrix products, arithmetic and copies ran while one was open for 1% of the time, Pallas kernels for 0%

commit v1 on v0

--- a/solution.py
+++ b/solution.py
@@ -113,7 +113,9 @@
     columns = z_forward(spread_entries(orbitals, own_selector), whole_cos, whole_sin)
     planes_columns = lax.all_to_all(columns, "ga", split_axis=3, concat_axis=2, tiled=True)
     gathered = plane_work(planes_columns, x_cos, x_sin, potential)
-    returned = lax.all_to_all(gathered, "ga", split_axis=2, concat_axis=3, tiled=True)
+    pieces = jnp.split(gathered, lax.axis_size("ga"), axis=2)
+    arrived = lax.all_to_all(jnp.stack(pieces), "ga", 0, 0)
+    returned = jnp.concatenate(arrived, axis=3)
     spectra = z_backward(returned, whole_cos, whole_sin, points)
     applied = pick_entries(spectra, own_selector)
     kinetic = kinetic_factor(own_sticks, own_lists, radius)

time: 107 us -> 107 us (level)
  local copies, waits for them, and re-layouts: 6.1 us -> 4.79 us
    unnamed x10 -> x9, local copies, waits for them, and re-layouts: 2.18 us -> 2.01 us
where the time goes in v1:
time: 107 us; the launch traced here: 106 us
  blocking collectives  46.5 us (43%)
  matrix products  37 us (35%)
  starting transfers between devices  7.82 us (7%)
  waiting for transfers between devices  6.46 us (6%)
  local copies, waits for them, and re-layouts  4.79 us (4%)
  other arithmetic  2.56 us (2%)
    all_gather x1, blocking collectives, body(): portion = lax.all_gather(masked, 'band', axis=1, tiled=True)  24.4 us
    all_gather x1, blocking collectives, body(): matrices = lax.all_gather(summed, 'band', axis=3, tiled=True)  17.2 us
    all_to_all x1, waiting for transfers between devices, body(): arrived = lax.all_to_all(jnp.stack(pieces), 'ga', 0, 0)  6.46 us
    dot_general x1, matrix products, pick_entries(): jnp.einsum('cbsp,skp->cbsk', spectra, selector.astype(jnp.float32), preci...  5.62 us
    psum x1, blocking collectives, body(): summed = lax.psum(block, 'ga')  4.93 us
    all_to_all x1, starting transfers between devices, body(): lax.all_to_all(columns, 'ga', split_axis=3, concat_axis=2, tiled=True)  4.36 us
    all_to_all x1, starting transfers between devices, body(): arrived = lax.all_to_all(jnp.stack(pieces), 'ga', 0, 0)  3.45 us
    dot_general x1, matrix products, spread_entries(): jnp.einsum('cbsk,skp->cbsp', coeffs, selector, preferred_element_type=jnp...  3.01 us
  transfers between devices with their start and end apart: 2, of which 1 were waited for; matrix products, arithmetic and copies ran while one was open for 1% of the time, Pallas kernels for 0%

profile of v1, /device:TPU:0, one launch (start us, length us, event | category | flops | bytes accessed | tf_op | source)
XLA Modules:
  0.0 106.1 jit_solution(2580247552078738242)
XLA Ops:
  0.6 0.8 add_multiply_fusion
  1.4 0.9 convert_multiply_fusion
  2.3 3.0 %fusion.10 = f32[2,1,80,128]{3,0,2,1:T(2,128)S(1)} fusion(s32[80,128]{1,0:T(8,128)S(1)} %get-tuple-element.16, bf16[2,80,128]{2,1,0:T(8,128)(2,1)} %bitcast.160), kind=kOutput, calls=%fused_computation.17 | convolution fusion | flops 6553600 | bytes 163840 | tf_op jit(solution)/shard_map/cbsk,skp->cbsp/dot_general | solution.py:31
  5.3 0.1 fusion.197
  5.3 1.3 %fusion.54 = f32[80,480]{1,0:T(8,128)S(1)} fusion(f32[80,128]{1,0:T(8,128)S(1)} %bitcast.158, s32[128]{0:T(128)S(1)} %iota_add_fusion), kind=kOutput, calls=%fused_computation.79 | convolution fusion | flops 59535360 | bytes 195072 | tf_op jit(solution)/shard_map/bsp,pz->bsz/dot_general | solution.py:41
  6.7 1.4 %fusion.58 = f32[80,480]{1,0:T(8,128)S(1)} fusion(f32[80,128]{1,0:T(8,128)S(1)} %bitcast.159, s32[128]{0:T(128)S(1)} %iota_add_fusion), kind=kOutput, calls=%fused_computation.80 | convolution fusion | flops 59535360 | bytes 195072 | tf_op jit(solution)/shard_map/bsp,pz->bsz/dot_general | solution.py:44
  8.1 1.4 %fusion.9 = f32[1,1,80,480]{3,2,1,0:T(8,128)S(1)} fusion(f32[80,480]{1,0:T(8,128)S(1)} %fusion.54, f32[80,128]{1,0:T(8,128)S(1)} %bitcast.156, s32[128]{0:T(128)S(1)} %iota_add_fusion), kind=kOutput, calls=%fused_computation.16 | convolution fusion | flops 59573760 | bytes 348672 | tf_op jit(solution)/shard_map/bsp,pz->bsz/dot_general | solution.py:43
  9.5 1.4 %fusion.8 = f32[1,1,80,480]{3,2,1,0:T(8,128)S(1)} fusion(f32[80,480]{1,0:T(8,128)S(1)} %fusion.58, f32[80,128]{1,0:T(8,128)S(1)} %bitcast.157, s32[128]{0:T(128)S(1)} %iota_add_fusion), kind=kOutput, calls=%fused_computation.14 | convolution fusion | flops 59573760 | bytes 348672 | tf_op jit(solution)/shard_map/bsp,pz->bsz/dot_general | solution.py:46
  10.8 1.0 copy.41
  11.9 4.4 %all-to-all-start = ((f32[2,1,80,480]{2,1,0,3:T(1,128)}), f32[2,1,80,480]{2,1,0,3:T(1,128)S(1)}, u32[]{:S(2)}, u32[]{:S(2)}) async-start(f32[2,1,80,480]{2,1,0,3:T(1,128)} %copy.41), calls=%async_computation | async-start | bytes 983040 | tf_op jit(solution)/shard_map/all_to_all | solution.py:114
  16.3 0.1 broadcast_select_fusion
  16.4 24.4 %all_gather.6 = bf16[2,16,80,128]{3,2,0,1:T(8,128)(2,1)S(1)} all-gather(bf16[2,1,80,128]{3,2,0,1:T(8,128)(2,1)S(1)} %copy.50), channel_id=1, replica_groups=mesh['band'=16,'ga'=2] {'band'}, dimensions={1}, use_global_device_ids=true | all-gather | bytes 696320 | tf_op jit(solution)/shard_map/all_gather | solution.py:130
  40.8 0.2 convolution_bitcast_fusion.5
  41.1 0.2 fusion.22
  41.3 0.8 copy.55
  42.1 0.1 fusion.196
  42.3 1.9 %fusion.42 = f32[240,480]{1,0:T(8,128)S(1)} fusion(f32[160,240]{1,0:T(8,128)S(1)} %bitcast.154, f32[160]{0:T(256)S(1)} %compare_convert_fusion, s32[160]{0:T(256)S(1)} %broadcast_add_fusion), kind=kOutput, calls=%fused_computation.69 | convolution fusion | flops 221952000 | bytes 615680 | tf_op jit(solution)/shard_map/bsz,sx->bzx/dot_general | solution.py:54
  44.2 0.0 copy-start
  44.2 1.9 %fusion.41 = f32[240,480]{1,0:T(8,128)S(1)} fusion(f32[160,240]{1,0:T(8,128)S(1)} %bitcast.155, f32[160]{0:T(256)S(1)} %compare_convert_fusion, s32[160]{0:T(256)S(1)} %broadcast_add_fusion), kind=kOutput, calls=%fused_computation.68 | convolution fusion | flops 221952000 | bytes 615680 | tf_op jit(solution)/shard_map/bsz,sx->bzx/dot_general | solution.py:51
  46.1 1.9 %fusion.4 = f32[240,480]{1,0:T(8,128)S(1)} fusion(f32[240,480]{1,0:T(8,128)S(1)} %copy-done, f32[240,480]{1,0:T(8,128)S(1)} %fusion.42, f32[160,240]{1,0:T(8,128)S(1)} %bitcast.142, f32[160]{0:T(256)S(1)} %compare_convert_fusion, s32[160]{0:T(256)S(1)} %broadcast_add_fusion), kind=kOutput, calls=%fused_computation.6 | convolution fusion | flops 222182400 | bytes 1537280 | tf_op jit(solution)/shard_map/bsz,sx->bzx/dot_general | solution.py:56
  48.0 1.9 %fusion.39 = f32[160,240]{1,0:T(8,128)S(1)} fusion(f32[240,480]{1,0:T(8,128)S(1)} %fusion.4, f32[160]{0:T(256)S(1)} %compare_convert_fusion, s32[160]{0:T(256)S(1)} %broadcast_add_fusion), kind=kOutput, calls=%fused_computation.66 | convolution fusion | flops 221952000 | bytes 615680 | tf_op jit(solution)/shard_map/bzx,sx->bsz/dot_general | solution.py:62
  49.9 1.9 %fusion.5 = f32[240,480]{1,0:T(8,128)S(1)} fusion(f32[240,480]{1,0:T(8,128)S(1)} %copy-done, f32[240,480]{1,0:T(8,128)S(1)} %fusion.41, f32[160,240]{1,0:T(8,128)S(1)} %bitcast.143, f32[160]{0:T(256)S(1)} %compare_convert_fusion, s32[160]{0:T(256)S(1)} %broadcast_add_fusion), kind=kOutput, calls=%fused_computation.8 | convolution fusion | flops 222182400 | bytes 1537280 | tf_op jit(solution)/shard_map/bsz,sx->bzx/dot_general | solution.py:53
  51.8 1.9 %fusion.40 = f32[160,240]{1,0:T(8,128)S(1)} fusion(f32[240,480]{1,0:T(8,128)S(1)} %fusion.5, f32[160]{0:T(256)S(1)} %compare_convert_fusion, s32[160]{0:T(256)S(1)} %broadcast_add_fusion), kind=kOutput, calls=%fused_computation.67 | convolution fusion | flops 221952000 | bytes 615680 | tf_op jit(solution)/shard_map/bzx,sx->bsz/dot_general | solution.py:59
  53.7 2.1 %fusion.6 = f32[1,1,160,240]{3,2,1,0:T(8,128)S(1)} fusion(f32[160,240]{1,0:T(8,128)S(1)} %fusion.39, f32[240,480]{1,0:T(8,128)S(1)} %fusion.5, f32[160]{0:T(256)S(1)} %compare_convert_fusion, s32[160]{0:T(256)S(1)} %broadcast_add_fusion), kind=kOutput, calls=%fused_computation.10 | convolution fusion | flops 221990400 | bytes 769280 | tf_op jit(solution)/shard_map/bzx,sx->bsz/dot_general | solution.py:64
  55.9 1.9 %fusion.7 = f32[1,1,160,240]{3,2,1,0:T(8,128)S(1)} fusion(f32[160,240]{1,0:T(8,128)S(1)} %fusion.40, f32[240,480]{1,0:T(8,128)S(1)} %fusion.4, f32[160]{0:T(256)S(1)} %compare_convert_fusion, s32[160]{0:T(256)S(1)} %broadcast_add_fusion), kind=kOutput, calls=%fused_computation.12 | convolution fusion | flops 221990400 | bytes 769280 | tf_op jit(solution)/shard_map/bzx,sx->bsz/dot_general | solution.py:61
  57.9 0.7 pad_maximum_fusion.2
  58.6 3.5 %all-to-all-start.1 = ((f32[2,2,1,80,240]{4,3,1,2,0:T(8,128)}), f32[2,2,1,80,240]{4,3,1,2,0:T(8,128)S(1)}, u32[]{:S(2)}, u32[]{:S(2)}) async-start(f32[2,2,1,80,240]{4,3,1,2,0:T(8,128)} %pad_maximum_fusion.2), calls=%async_computation.1 | async-start | bytes 655360 | tf_op jit(solution)/shard_map/all_to_all | solution.py:117
  62.1 0.2 convolution_bitcast_fusion.7
  62.3 0.2 fusion.24
  62.5 6.5 %all-to-all-done.1 = f32[2,2,1,80,240]{4,3,1,2,0:T(8,128)S(1)} async-done(((f32[2,2,1,80,240]{4,3,1,2,0:T(8,128)}), f32[2,2,1,80,240]{4,3,1,2,0:T(8,128)S(1)}, u32[]{:S(2)}, u32[]{:S(2)}) %all-to-all-start.1) | async-done | bytes 307232 | tf_op jit(solution)/shard_map/all_to_all | solution.py:117
  69.0 0.1 copy.46
  69.1 0.2 reshape.272
  69.3 1.4 %fusion.51 = f32[80,128]{1,0:T(8,128)S(1)} fusion(f32[80,480]{1,0:T(8,128)S(1)} %reshape.272, s32[128]{0:T(128)S(1)} %iota_add_fusion), kind=kOutput, calls=%fused_computation.78 | convolution fusion | flops 59535360 | bytes 195072 | tf_op jit(solution)/shard_map/bsz,pz->bsp/dot_general | solution.py:69
  70.8 0.1 copy.47
  70.9 0.2 reshape.273
  71.1 1.4 %fusion.49 = f32[80,128]{1,0:T(8,128)S(1)} fusion(f32[80,480]{1,0:T(8,128)S(1)} %reshape.273, s32[128]{0:T(128)S(1)} %iota_add_fusion), kind=kOutput, calls=%fused_computation.77 | convolution fusion | flops 59535360 | bytes 195072 | tf_op jit(solution)/shard_map/bsz,pz->bsp/dot_general | solution.py:72
  72.5 1.4 %fusion.16 = f32[1,80,128]{2,1,0:T(8,128)S(1)} fusion(f32[80,128]{1,0:T(8,128)S(1)} %fusion.51, f32[80,480]{1,0:T(8,128)S(1)} %reshape.273, s32[128]{0:T(128)S(1)} %iota_add_fusion), kind=kOutput, calls=%fused_computation.25 | convolution fusion | flops 59545600 | bytes 236032 | tf_op jit(solution)/shard_map/bsz,pz->bsp/dot_general | solution.py:71
  73.9 1.5 %fusion.15 = f32[1,80,128]{2,1,0:T(8,128)S(1)} fusion(f32[80,128]{1,0:T(8,128)S(1)} %fusion.49, f32[80,480]{1,0:T(8,128)S(1)} %reshape.272, s32[128]{0:T(128)S(1)} %iota_add_fusion), kind=kOutput, calls=%fused_computation.23 | convolution fusion | flops 59545600 | bytes 236032 | tf_op jit(solution)/shard_map/bsz,pz->bsp/dot_general | solution.py:74
  75.4 5.6 %fusion.14 = bf16[2,1,80,128]{3,0,2,1:T(2,128)(2,1)S(1)} fusion(s32[80,128]{1,0:T(8,128)S(1)} %get-tuple-element.16, f32[2,80,128]{2,1,0:T(8,128)S(1)} %maximum_multiply_fusion, pred[80,128]{1,0:T(8,128)(4,1)S(1)} %broadcast_compare_fusion, f32[80,128]{1,0:T(8,128)S(1)} %get-tuple-element.15, bf16[2,1,80,128]{3,2,1,0:T(8,128)(2,1)S(1)} %copy-done.1), kind=kOutput, calls=%fused_computation.21 | convolution fusion | flops 32870400 | bytes 256000 | tf_op jit(solution)/shard_map/cbsp,skp->cbsk/dot_general | solution.py:35
  81.0 0.2 convolution_bitcast_fusion.3
  81.3 0.2 convolution_bitcast_fusion.1
  81.5 0.6 copy.52
  82.1 0.2 fusion.20
  82.3 0.2 fusion.18
  82.6 4.9 %psum.7 = f32[2,2,16,1]{2,3,1,0:T(1,128)S(1)} all-reduce(f32[2,2,16,1]{2,3,1,0:T(1,128)S(1)} %pad_maximum_fusion.3), channel_id=1, replica_groups=mesh['band'=16,'ga'=2] {'ga'}, use_global_device_ids=true, to_apply=%region_0.1 | all-reduce | flops 64 | bytes 512 | tf_op jit(solution)/shard_map/psum | solution.py:135
  87.5 17.2 %all_gather.7 = f32[2,2,16,16]{2,1,0,3:T(2,128)S(1)} all-gather(f32[2,2,16,1]{2,1,0,3:T(2,128)S(1)} %bitcast.161), channel_id=1, replica_groups=mesh['band'=16,'ga'=2] {'band'}, dimensions={3}, use_global_device_ids=true | all-gather | bytes 4352 | tf_op jit(solution)/shard_map/all_gather | solution.py:136
  104.7 0.7 copy.53
  105.4 0.7 copy.54
  (23 shorter events, 0.3 us)
Async XLA Ops:
  11.9 4.4 %copy-start.2 = (s32[160]{0:T(256)S(1)}, s32[160]{0:T(256)}, u32[]{:S(2)}) copy-start(s32[160]{0:T(256)} %param.6) | copy-start | bytes 1924
  11.9 4.4 %copy-start.1 = (bf16[2,1,80,128]{3,2,1,0:T(8,128)(2,1)S(1)}, bf16[2,1,80,128]{3,2,1,0:T(8,128)(2,1)}, u32[]{:S(2)}) copy-start(bf16[2,1,80,128]{3,2,1,0:T(8,128)(2,1)} %param.4) | copy-start | bytes 122884
  11.9 29.4 %all-to-all-start = ((f32[2,1,80,480]{2,1,0,3:T(1,128)}), f32[2,1,80,480]{2,1,0,3:T(1,128)S(1)}, u32[]{:S(2)}, u32[]{:S(2)}) async-start(f32[2,1,80,480]{2,1,0,3:T(1,128)} %copy.41), calls=%async_computation | async-start | bytes 983040 | tf_op jit(solution)/shard_map/all_to_all | solution.py:114
  44.2 1.9 %copy-start = (f32[240,480]{1,0:T(8,128)S(1)}, f32[240,480]{1,0:T(8,128)}, u32[]{:S(2)}) copy-start(f32[240,480]{1,0:T(8,128)} %param.5) | copy-start | bytes 1382404
  58.6 10.4 %all-to-all-start.1 = ((f32[2,2,1,80,240]{4,3,1,2,0:T(8,128)}), f32[2,2,1,80,240]{4,3,1,2,0:T(8,128)S(1)}, u32[]{:S(2)}, u32[]{:S(2)}) async-start(f32[2,2,1,80,240]{4,3,1,2,0:T(8,128)} %pad_maximum_fusion.2), calls=%async_computation.1 | async-start | bytes 655360 | tf_op jit(solution)/shard_map/all_to_all | solution.py:117
